TPU v7x, 128 devices: a whole 4x4x4 slice. The times are simulated.
128 devices in a mesh: src: 16 (over y, z), reg: 8 (over x, core).
Axes of the slice: x: 4, y: 4, z: 4, core: 2. Of those that a mesh axis runs over, the one named last changes fastest.
Arguments:
- tiles: bfloat16 [65536, 128, 128], P(('src', 'reg')), may hold values from -0.1875 to 0.1875
- rays: float32 [8192, 128], P(('src', 'reg')), may hold values from -6 to 6
- tile_rows: int32 [65536], P(('src', 'reg')), may hold values from 0 to 63, as said below
- tile_slots: int32 [65536], P(('src', 'reg')), may hold values from 0 to 255, as said below
- tile_count: int32 [128], P(('src', 'reg')), may hold values from 256 to 512, as said below
- wanted: int32 [128, 128, 2], P(('src', 'reg')), may hold values from 0 to 255
Outputs:
- solution: float32 [32768, 128], P(('src', 'reg'))
- right_vector: float32 [32768, 128], P(('src', 'reg'))
Inputs may be any that keep to these rules, and one draw needn't show every extreme that they name: `tile_rows`: non-decreasing along each device's 512 tiles. `tile_slots`: the first 256 tiles of each device name every slot once. `tile_count`: some device has all 512 tiles live.
All inputs are finite; a program needn't handle non-finite values.
Results may differ from a plain program's by a relative error of at most 0.024.
Values may be sent and summed in bfloat16 or wider, within the bound.
A program may use at most 128 MiB of HBM per device.

v0:
```python
import jax
import jax.numpy as jnp
from jax import lax
from jax.sharding import Mesh
from jax.sharding import PartitionSpec as P

BLK_DEV = 256
ITERS = 3
SRC_REG = ("src_0", "src_1", "reg_0", "reg_1")


damping = 0.5


def over_axes(value, axes):
    for axis in axes:
        value = lax.psum(value, axis)
    return value


def per_device(tiles, rays, tile_rows, tile_slots, tile_count, wanted):
    device_list = lax.axis_size(SRC_REG)
    width = tiles.shape[2]
    row_blocks = rays.shape[0]
    cap = wanted.shape[2]
    requests = wanted[0].reshape(-1)
    live = (jnp.arange(tiles.shape[0], dtype=jnp.int32) < tile_count[0]).astype(jnp.float32)[
        :, None
    ]
    u = jnp.zeros_like(rays)
    v = jnp.zeros((BLK_DEV, width), jnp.float32)
    solution = jnp.zeros((BLK_DEV, width), jnp.float32)
    w = jnp.zeros((BLK_DEV, width), jnp.float32)
    uraw = rays
    vraw = v
    alpha = jnp.float32(1.0)
    phibar = jnp.float32(0.0)
    rhobar = jnp.float32(0.0)
    for step in range(ITERS + 1):
        if step > 0:
            outgoing = vraw.astype(jnp.bfloat16)[requests].reshape(device_list, cap, width)
            incoming = lax.all_to_all(outgoing, SRC_REG, split_axis=0, concat_axis=0, tiled=True)
            fetched = incoming.reshape(device_list * cap, width)
            forward_picked = fetched[tile_slots]
            product = (
                jnp.einsum("tij,tj->ti", tiles, forward_picked, preferred_element_type=jnp.float32)
                * live
            )
            uraw = (
                jax.ops.segment_sum(product, tile_rows, num_segments=row_blocks) / alpha - alpha * u
            )
        picked = uraw.astype(jnp.bfloat16)[tile_rows]
        contrib = jnp.einsum("tij,ti->tj", tiles, picked, preferred_element_type=jnp.float32) * live
        adjoint_slot_sums = jax.ops.segment_sum(contrib, tile_slots, num_segments=device_list * cap)
        slot_sums = adjoint_slot_sums.reshape(device_list, cap, width)
        returned = lax.all_to_all(
            slot_sums.astype(jnp.bfloat16), SRC_REG, split_axis=0, concat_axis=0, tiled=True
        ).astype(slot_sums.dtype)
        adjoint_returned = returned.reshape(device_list * cap, width)
        grad = jax.ops.segment_sum(adjoint_returned, requests, num_segments=BLK_DEV)
        sum_uu, sum_pp, sum_pv, sum_vv = (
            over_axes(jnp.sum(uraw * uraw), SRC_REG),
            over_axes(jnp.sum(grad * grad), SRC_REG),
            over_axes(jnp.sum(grad * v), SRC_REG),
            over_axes(jnp.sum(v * v), SRC_REG),
        )
        beta = jnp.sqrt(sum_uu)
        vraw = grad / beta - beta * v
        alpha_new = jnp.sqrt(sum_pp / sum_uu - 2.0 * sum_pv + sum_uu * sum_vv)
        u = uraw / beta
        v_new = vraw / alpha_new
        if step == 0:
            w = v_new
            phibar = beta
            rhobar = alpha_new
        else:
            rhobar1 = jnp.sqrt(rhobar * rhobar + damping * damping)
            phibar = rhobar / rhobar1 * phibar
            rho = jnp.sqrt(rhobar1 * rhobar1 + beta * beta)
            cosine = rhobar1 / rho
            sine = beta / rho
            theta = sine * alpha_new
            rhobar = -cosine * alpha_new
            phi = cosine * phibar
            phibar = sine * phibar
            solution = solution + phi / rho * w
            w = v_new - theta / rho * w
        v = v_new
        alpha = alpha_new
    scale = jnp.sqrt(jnp.float32(BLK_DEV * width * device_list))
    return (solution, v * scale)


def solution(mesh):
    split = Mesh(mesh.devices.reshape(4, 4, 4, 2), ("src_0", "src_1", "reg_0", "reg_1"))
    placed = (
        P(SRC_REG, None, None),
        P(SRC_REG, None),
        P(SRC_REG),
        P(SRC_REG),
        P(SRC_REG),
        P(SRC_REG, None, None),
    )
    return jax.shard_map(
        per_device,
        mesh=split,
        in_specs=placed,
        out_specs=(P(SRC_REG, None), P(SRC_REG, None)),
        check_vma=False,
    )
```

profile of v0, /device:TPU:1, one launch (start us, length us, event | category | flops | bytes accessed | tf_op | source)
XLA Modules:
  0.0 359.4 jit_solution(1995274523629218105)
XLA Ops:
  4.8 8.1 %fusion.12 = f32[512,1,128]{2,1,0:T(1,128)S(1)} fusion(bf16[512,128,128]{2,1,0:T(8,128)(2,1)} %param.6, bf16[512,128,1]{1,0,2:T(8,128)(2,1)S(1)} %bitcast.59), kind=kOutput, calls=%fused_computation.33 | convolution fusion | flops 16777216 | bytes 17170432 | tf_op jit(solution)/shard_map/tij,ti->tj/dot_general | solution.py:53
  15.9 11.5 %all-to-all-start = ((bf16[128,2,128]{2,1,0:T(2,128)(2,1)}), bf16[128,2,128]{2,1,0:T(2,128)(2,1)S(1)}, u32[]{:S(2)}, u32[]{:S(2)}) async-start(bf16[128,2,128]{2,1,0:T(2,128)(2,1)} %bitcast.4), calls=%async_computation | async-start | bytes 131072 | tf_op jit(solution)/shard_map/all_to_all | solution.py:56
  27.9 9.0 %all-to-all-done = bf16[128,2,128]{2,1,0:T(2,128)(2,1)S(1)} async-done(((bf16[128,2,128]{2,1,0:T(2,128)(2,1)}), bf16[128,2,128]{2,1,0:T(2,128)(2,1)S(1)}, u32[]{:S(2)}, u32[]{:S(2)}) %all-to-all-start) | async-done | bytes 65568 | tf_op jit(solution)/shard_map/all_to_all | solution.py:56
  39.0 8.0 %all-reduce.11 = (f32[]{:T(128)}, f32[]{:T(128)}, f32[]{:T(128)}, f32[]{:T(128)}) all-reduce(f32[]{:T(128)} %get-tuple-element.12, f32[]{:T(128)} %get-tuple-element.87, f32[]{:T(128)} %get-tuple-element.11, f32[]{:T(128)} %constant.7.clone.1), channel_id=1, replica_groups=mesh['src_0'=4,'src_1'=4,'reg_0'=4,'reg_1'=2] {'src_0'}, use_global_device_ids=true, to_apply=%region_3.0 | all-reduce | flops 4 | bytes 32 | tf_op jit(solution)/shard_map/psum | solution.py:17
  54.5 7.6 %all-reduce.3 = (f32[]{:T(128)}, f32[]{:T(128)}, f32[]{:T(128)}, f32[]{:T(128)}) all-reduce(f32[]{:T(128)} %get-tuple-element.41, f32[]{:T(128)} %get-tuple-element.42, f32[]{:T(128)} %get-tuple-element.43, f32[]{:T(128)} %get-tuple-element.44), channel_id=1, replica_groups=mesh['src_0'=4,'src_1'=4,'reg_0'=4,'reg_1'=2] {'reg_0'}, use_global_device_ids=true, to_apply=%region_5.0 | all-reduce | flops 4 | bytes 32 | tf_op jit(solution)/shard_map/psum | solution.py:17
  62.1 9.5 %all-reduce.15 = (f32[]{:T(128)}, f32[]{:T(128)}, f32[]{:T(128)}, f32[]{:T(128)}) all-reduce(f32[]{:T(128)} %get-tuple-element.25, f32[]{:T(128)} %get-tuple-element.26, f32[]{:T(128)} %get-tuple-element.27, f32[]{:T(128)} %get-tuple-element.28), channel_id=1, replica_groups=mesh['src_0'=4,'src_1'=4,'reg_0'=4,'reg_1'=2] {'reg_1'}, use_global_device_ids=true, to_apply=%region_6.0 | all-reduce | flops 4 | bytes 32 | tf_op jit(solution)/shard_map/psum | solution.py:17
  88.7 12.2 %fusion.10 = f32[512,1,128]{2,1,0:T(1,128)S(1)} fusion(bf16[512,128,128]{2,1,0:T(8,128)(2,1)} %param.6, bf16[512,128,1]{1,0,2:T(8,128)(2,1)S(1)} %bitcast.53), kind=kOutput, calls=%fused_computation.31 | convolution fusion | flops 16777216 | bytes 17170432 | tf_op jit(solution)/shard_map/tij,tj->ti/dot_general | solution.py:46
  107.0 8.1 %fusion.8 = f32[512,1,128]{2,1,0:T(1,128)S(1)} fusion(bf16[512,128,128]{2,1,0:T(8,128)(2,1)} %param.6, bf16[512,128,1]{1,0,2:T(8,128)(2,1)S(1)} %bitcast.60), kind=kOutput, calls=%fused_computation.29 | convolution fusion | flops 16777216 | bytes 17170432 | tf_op jit(solution)/shard_map/tij,ti->tj/dot_general | solution.py:53
  117.5 13.9 %all_to_all.35 = bf16[128,2,128]{2,1,0:T(2,128)(2,1)S(1)} all-to-all(bf16[128,2,128]{2,1,0:T(2,128)(2,1)S(1)} %bitcast.68), channel_id=1, replica_groups=mesh['src_0'=4,'src_1'=4,'reg_0'=4,'reg_1'=2] {'src_0','src_1','reg_0','..., dimensions={0} | all-to-all | bytes 131072 | tf_op jit(solution)/shard_map/all_to_all | solution.py:56
  133.7 7.5 %all-reduce.10 = (f32[]{:T(128)}, f32[]{:T(128)}, f32[]{:T(128)}, f32[]{:T(128)}) all-reduce(f32[]{:T(128)} %get-tuple-element.10, f32[]{:T(128)} %get-tuple-element.83, f32[]{:T(128)} %get-tuple-element.9, f32[]{:T(128)} %get-tuple-element.8), channel_id=1, replica_groups=mesh['src_0'=4,'src_1'=4,'reg_0'=4,'reg_1'=2] {'src_0'}, use_global_device_ids=true, to_apply=%region_30.0 | all-reduce | flops 4 | bytes 32 | tf_op jit(solution)/shard_map/psum | solution.py:17
  148.6 7.6 %all-reduce.2 = (f32[]{:T(128)}, f32[]{:T(128)}, f32[]{:T(128)}, f32[]{:T(128)}) all-reduce(f32[]{:T(128)} %get-tuple-element.37, f32[]{:T(128)} %get-tuple-element.38, f32[]{:T(128)} %get-tuple-element.39, f32[]{:T(128)} %get-tuple-element.40), channel_id=1, replica_groups=mesh['src_0'=4,'src_1'=4,'reg_0'=4,'reg_1'=2] {'reg_0'}, use_global_device_ids=true, to_apply=%region_32.0 | all-reduce | flops 4 | bytes 32 | tf_op jit(solution)/shard_map/psum | solution.py:17
  156.2 9.5 %all-reduce.14 = (f32[]{:T(128)}, f32[]{:T(128)}, f32[]{:T(128)}, f32[]{:T(128)}) all-reduce(f32[]{:T(128)} %get-tuple-element.21, f32[]{:T(128)} %get-tuple-element.22, f32[]{:T(128)} %get-tuple-element.23, f32[]{:T(128)} %get-tuple-element.24), channel_id=1, replica_groups=mesh['src_0'=4,'src_1'=4,'reg_0'=4,'reg_1'=2] {'reg_1'}, use_global_device_ids=true, to_apply=%region_33.0 | all-reduce | flops 4 | bytes 32 | tf_op jit(solution)/shard_map/psum | solution.py:17
  182.8 12.2 %fusion.6 = f32[512,1,128]{2,1,0:T(1,128)S(1)} fusion(bf16[512,128,128]{2,1,0:T(8,128)(2,1)} %param.6, bf16[512,128,1]{1,0,2:T(8,128)(2,1)S(1)} %bitcast.54), kind=kOutput, calls=%fused_computation.27 | convolution fusion | flops 16777216 | bytes 17170432 | tf_op jit(solution)/shard_map/tij,tj->ti/dot_general | solution.py:46
  201.1 8.1 %fusion.4 = f32[512,1,128]{2,1,0:T(1,128)S(1)} fusion(bf16[512,128,128]{2,1,0:T(8,128)(2,1)} %param.6, bf16[512,128,1]{1,0,2:T(8,128)(2,1)S(1)} %bitcast.61), kind=kOutput, calls=%fused_computation.25 | convolution fusion | flops 16777216 | bytes 17170432 | tf_op jit(solution)/shard_map/tij,ti->tj/dot_general | solution.py:53
  211.6 13.9 %all_to_all.36 = bf16[128,2,128]{2,1,0:T(2,128)(2,1)S(1)} all-to-all(bf16[128,2,128]{2,1,0:T(2,128)(2,1)S(1)} %bitcast.70), channel_id=1, replica_groups=mesh['src_0'=4,'src_1'=4,'reg_0'=4,'reg_1'=2] {'src_0','src_1','reg_0','..., dimensions={0} | all-to-all | bytes 131072 | tf_op jit(solution)/shard_map/all_to_all | solution.py:56
  227.7 7.5 %all-reduce.9 = (f32[]{:T(128)}, f32[]{:T(128)}, f32[]{:T(128)}, f32[]{:T(128)}) all-reduce(f32[]{:T(128)} %get-tuple-element.7, f32[]{:T(128)} %get-tuple-element.80, f32[]{:T(128)} %get-tuple-element.6, f32[]{:T(128)} %get-tuple-element.5), channel_id=1, replica_groups=mesh['src_0'=4,'src_1'=4,'reg_0'=4,'reg_1'=2] {'src_0'}, use_global_device_ids=true, to_apply=%region_53.0 | all-reduce | flops 4 | bytes 32 | tf_op jit(solution)/shard_map/psum | solution.py:17
  242.7 7.6 %all-reduce.1 = (f32[]{:T(128)}, f32[]{:T(128)}, f32[]{:T(128)}, f32[]{:T(128)}) all-reduce(f32[]{:T(128)} %get-tuple-element.33, f32[]{:T(128)} %get-tuple-element.34, f32[]{:T(128)} %get-tuple-element.35, f32[]{:T(128)} %get-tuple-element.36), channel_id=1, replica_groups=mesh['src_0'=4,'src_1'=4,'reg_0'=4,'reg_1'=2] {'reg_0'}, use_global_device_ids=true, to_apply=%region_55.0 | all-reduce | flops 4 | bytes 32 | tf_op jit(solution)/shard_map/psum | solution.py:17
  250.3 9.7 %all-reduce.13 = (f32[]{:T(128)}, f32[]{:T(128)}, f32[]{:T(128)}, f32[]{:T(128)}) all-reduce(f32[]{:T(128)} %get-tuple-element.17, f32[]{:T(128)} %get-tuple-element.18, f32[]{:T(128)} %get-tuple-element.19, f32[]{:T(128)} %get-tuple-element.20), channel_id=1, replica_groups=mesh['src_0'=4,'src_1'=4,'reg_0'=4,'reg_1'=2] {'reg_1'}, use_global_device_ids=true, to_apply=%region_56.0 | all-reduce | flops 4 | bytes 32 | tf_op jit(solution)/shard_map/psum | solution.py:17
  276.9 12.2 %fusion.2 = f32[512,1,128]{2,1,0:T(1,128)S(1)} fusion(bf16[512,128,128]{2,1,0:T(8,128)(2,1)} %param.6, bf16[512,128,1]{1,0,2:T(8,128)(2,1)S(1)} %bitcast.52), kind=kOutput, calls=%fused_computation.23 | convolution fusion | flops 16777216 | bytes 17170432 | tf_op jit(solution)/shard_map/tij,tj->ti/dot_general | solution.py:46
  294.6 8.1 %fusion = f32[512,1,128]{2,1,0:T(1,128)S(1)} fusion(bf16[512,128,128]{2,1,0:T(8,128)(2,1)} %param.6, bf16[512,128,1]{1,0,2:T(8,128)(2,1)S(1)} %bitcast.58), kind=kOutput, calls=%fused_computation.21 | convolution fusion | flops 16777216 | bytes 17170432 | tf_op jit(solution)/shard_map/tij,ti->tj/dot_general | solution.py:53
  311.0 8.8 %all-to-all-done.6 = bf16[128,2,128]{2,1,0:T(2,128)(2,1)S(1)} async-done(((bf16[128,2,128]{2,1,0:T(2,128)(2,1)}), bf16[128,2,128]{2,1,0:T(2,128)(2,1)S(1)}, u32[]{:S(2)}, u32[]{:S(2)}) %all-to-all-start.6) | async-done | bytes 65568 | tf_op jit(solution)/shard_map/all_to_all | solution.py:56
  322.0 7.5 %all-reduce.8 = (f32[]{:T(128)}, f32[]{:T(128)}, f32[]{:T(128)}, f32[]{:T(128)}) all-reduce(f32[]{:T(128)} %multiply_reduce_fusion.11, f32[]{:T(128)} %get-tuple-element.4, f32[]{:T(128)} %get-tuple-element.3, f32[]{:T(128)} %get-tuple-element.2), channel_id=1, replica_groups=mesh['src_0'=4,'src_1'=4,'reg_0'=4,'reg_1'=2] {'src_0'}, use_global_device_ids=true, to_apply=%region_69.0 | all-reduce | flops 4 | bytes 32 | tf_op jit(solution)/shard_map/psum | solution.py:17
  336.9 7.6 %all-reduce = (f32[]{:T(128)}, f32[]{:T(128)}, f32[]{:T(128)}, f32[]{:T(128)}) all-reduce(f32[]{:T(128)} %get-tuple-element.29, f32[]{:T(128)} %get-tuple-element.30, f32[]{:T(128)} %get-tuple-element.31, f32[]{:T(128)} %get-tuple-element.32), channel_id=1, replica_groups=mesh['src_0'=4,'src_1'=4,'reg_0'=4,'reg_1'=2] {'reg_0'}, use_global_device_ids=true, to_apply=%region_71.0 | all-reduce | flops 4 | bytes 32 | tf_op jit(solution)/shard_map/psum | solution.py:17
  344.5 9.5 %all-reduce.12 = (f32[]{:T(128)}, f32[]{:T(128)}, f32[]{:T(128)}, f32[]{:T(128)}) all-reduce(f32[]{:T(128)} %get-tuple-element.13, f32[]{:T(128)} %get-tuple-element.14, f32[]{:T(128)} %get-tuple-element.15, f32[]{:T(128)} %get-tuple-element.16), channel_id=1, replica_groups=mesh['src_0'=4,'src_1'=4,'reg_0'=4,'reg_1'=2] {'reg_1'}, use_global_device_ids=true, to_apply=%region_72.0 | all-reduce | flops 4 | bytes 32 | tf_op jit(solution)/shard_map/psum | solution.py:17
  (67 shorter events, 115.6 us)
Async XLA Ops:
  0.6 12.2 %copy-start.1 = (s32[512]{0:T(512)S(1)}, s32[512]{0:T(512)}, u32[]{:S(2)}) copy-start(s32[512]{0:T(512)} %param.9) | copy-start | bytes 6148
  0.6 26.8 %copy-start.2 = (s32[1,128,2]{1,2,0:T(2,128)S(1)}, s32[1,128,2]{1,2,0:T(2,128)}, u32[]{:S(2)}) copy-start(s32[1,128,2]{1,2,0:T(2,128)} %param.11) | copy-start | bytes 3076
  15.9 20.9 %all-to-all-start = ((bf16[128,2,128]{2,1,0:T(2,128)(2,1)}), bf16[128,2,128]{2,1,0:T(2,128)(2,1)S(1)}, u32[]{:S(2)}, u32[]{:S(2)}) async-start(bf16[128,2,128]{2,1,0:T(2,128)(2,1)} %bitcast.4), calls=%async_computation | async-start | bytes 131072 | tf_op jit(solution)/shard_map/all_to_all | solution.py:56
  73.8 13.6 %all-to-all-start.1 = ((bf16[128,2,128]{2,1,0:T(2,128)(2,1)}), bf16[128,2,128]{2,1,0:T(2,128)(2,1)S(1)}, u32[]{:S(2)}, u32[]{:S(2)}) async-start(bf16[128,2,128]{2,1,0:T(2,128)(2,1)} %bitcast.7), calls=%async_computation.1 | async-start | bytes 131072 | tf_op jit(solution)/shard_map/all_to_all | solution.py:42
  88.7 16.3 %copy-start = (f32[64,128]{1,0:T(8,128)S(1)}, f32[64,128]{1,0:T(8,128)}, u32[]{:S(2)}) copy-start(f32[64,128]{1,0:T(8,128)} %param.7) | copy-start | bytes 98308
  167.9 13.5 %all-to-all-start.3 = ((bf16[128,2,128]{2,1,0:T(2,128)(2,1)}), bf16[128,2,128]{2,1,0:T(2,128)(2,1)S(1)}, u32[]{:S(2)}, u32[]{:S(2)}) async-start(bf16[128,2,128]{2,1,0:T(2,128)(2,1)} %bitcast.17), calls=%async_computation.3 | async-start | bytes 131072 | tf_op jit(solution)/shard_map/all_to_all | solution.py:42
  262.2 13.3 %all-to-all-start.5 = ((bf16[128,2,128]{2,1,0:T(2,128)(2,1)}), bf16[128,2,128]{2,1,0:T(2,128)(2,1)S(1)}, u32[]{:S(2)}, u32[]{:S(2)}) async-start(bf16[128,2,128]{2,1,0:T(2,128)(2,1)} %bitcast.27), calls=%async_computation.5 | async-start | bytes 131072 | tf_op jit(solution)/shard_map/all_to_all | solution.py:42
  305.7 14.1 %all-to-all-start.6 = ((bf16[128,2,128]{2,1,0:T(2,128)(2,1)}), bf16[128,2,128]{2,1,0:T(2,128)(2,1)S(1)}, u32[]{:S(2)}, u32[]{:S(2)}) async-start(bf16[128,2,128]{2,1,0:T(2,128)(2,1)} %bitcast.35), calls=%async_computation.6 | async-start | bytes 131072 | tf_op jit(solution)/shard_map/all_to_all | solution.py:56
where the time goes:
time: 366 us; the launch traced here: 359 us
  blocking collectives  157 us (43%)
  matrix products  68.9 us (19%)
  other arithmetic  37 us (10%)
  waiting for transfers between devices  36.1 us (10%)
  starting transfers between devices  27.8 us (8%)
  between operations  18.7 us (5%)
  local copies, waits for them, and re-layouts  14.2 us (4%)
    psum x16, blocking collectives, over_axes(): value = lax.psum(value, axis)  129 us
    dot_general x3, matrix products, per_device(): jnp.einsum('tij,tj->ti', tiles, forward_picked, preferred_element_type=jn...  36.6 us
    dot_general x4, matrix products, per_device(): jnp.einsum('tij,ti->tj', tiles, picked, preferred_element_type=jnp.float32)  32.3 us
    all_to_all x2, blocking collectives, per_device(): lax.all_to_all(slot_sums.astype(jnp.bfloat16), SRC_REG, split_axis=0, con...  27.9 us
    all_to_all x3, waiting for transfers between devices, per_device(): lax.all_to_all(outgoing, SRC_REG, split_axis=0, concat_axis=0, tiled=True)  18.3 us
    all_to_all x2, waiting for transfers between devices, per_device(): lax.all_to_all(slot_sums.astype(jnp.bfloat16), SRC_REG, split_axis=0, con...  17.8 us
    all_to_all x2, starting transfers between devices, per_device(): lax.all_to_all(slot_sums.astype(jnp.bfloat16), SRC_REG, split_axis=0, con...  16.1 us
    scatter-add x3, other arithmetic, per_device(): jax.ops.segment_sum(product, tile_rows, num_segments=row_blocks) / alpha  12.3 us
  transfers between devices with their start and end apart: 5, of which 5 were waited for; matrix products, arithmetic and copies ran while one was open for 0% of the time, Pallas kernels for 0%

commit v1 on v0

v1 whole, which is shorter than its diff:
```python
import jax
import jax.numpy as jnp
from jax import lax
from jax.experimental import pallas as pl
from jax.experimental.pallas import tpu as pltpu
from jax.sharding import Mesh
from jax.sharding import PartitionSpec as P

AXES = ("src_0", "src_1", "reg_0", "reg_1")
SIZES = (4, 4, 4, 2)
NDEV = 128
PEERS = NDEV - 1
BLK_DEV = 256
ITERS = 3
ROUNDS = 2 * ITERS + 2
NT = 512
TILE = 128
GROUP = 32
NG = NT // GROUP
MSG = 4
ROWS = NDEV * MSG
DAMPING = 0.5
BF = jnp.bfloat16
F32 = jnp.float32
MESH = pl.DeviceIdType.MESH


def peers_of(me):
    at = [
        [(me[axis] + off) % SIZES[axis] for off in range(SIZES[axis])] for axis in range(4)
    ]
    offsets = [
        (a, b, c, d) for a in range(4) for b in range(4) for c in range(4) for d in range(2)
    ]
    far = lambda o: -(min(o[0], 4 - o[0]) + min(o[1], 4 - o[1]) + min(o[2], 4 - o[2]) + o[3])
    offsets = sorted((o for o in offsets if any(o)), key=far)
    return [tuple(at[axis][o[axis]] for axis in range(4)) for o in offsets]


def index_of(place):
    return ((place[0] * 4 + place[1]) * 4 + place[2]) * 2 + place[3]


def split3(x):
    hi = x.astype(BF).astype(F32)
    mid = (x - hi).astype(BF).astype(F32)
    return hi, mid, x - hi - mid


def total(x):
    return jnp.sum(jnp.sum(x, axis=0, keepdims=True), axis=1, keepdims=True)


def split_store(ref, at, size, value):
    hi = value.astype(BF)
    ref[pl.ds(at, size), :TILE] = hi
    ref[pl.ds(at, size), TILE:] = (value - hi.astype(F32)).astype(BF)


def kernel(
    tiles_hbm, rays, idx, sol, right,
    tiles, picked, parts, s_slot, p_slot, s_row, q_row, comb, gath, uraw_r, u_r, v_r, vraw_r, w_r,
    send, recv, load_sem, send_sem, recv_sem,
):
    me = tuple(lax.axis_index(axis) for axis in AXES)
    mine = index_of(me)
    others = peers_of(me)

    def load(g):
        at = pl.ds(g * GROUP, GROUP)
        return pltpu.make_async_copy(tiles_hbm.at[at], tiles.at[at], load_sem.at[g])

    for g in range(NG):
        load(g).start()
    barrier = pltpu.get_barrier_semaphore()
    for place in others:
        pl.semaphore_signal(barrier, inc=1, device_id=place, device_id_type=MESH)

    iota = lambda shape, dim: lax.broadcasted_iota(jnp.int32, shape, dim)
    one, zero = jnp.ones((), BF), jnp.zeros((), BF)
    slots, rows, wanted, count = (idx[i : i + 1, :] for i in range(4))
    row_id = iota((ROWS, NT), 0)
    target = jnp.where(row_id % MSG < 2, (row_id // MSG) * 2 + row_id % MSG, -1)
    live_slots = jnp.where(iota((1, NT), 1) < count, slots, -2)
    hit = jnp.where(target == live_slots, 1.0, 0.0)
    s_slot[...] = hit.astype(BF)
    p_slot[...] = hit.T.astype(BF)
    hit = jnp.where(iota((64, NT), 0) == rows, 1.0, 0.0)
    s_row[...] = hit.astype(BF)
    hit = jnp.where(iota((TILE, NT), 0) == rows, 1.0, 0.0)
    q_row[...] = hit.T.astype(BF)
    hit = jnp.where(iota((BLK_DEV, ROWS), 0) == wanted, 1.0, 0.0)
    comb[...] = hit.astype(BF)
    gath[...] = hit.T.astype(BF)

    scalar_row = iota((ROWS, TILE), 0) % MSG == 2
    lane = iota((1, TILE), 1)
    scalar_mask = jnp.logical_and(scalar_row, iota((ROWS, TILE), 1) < 3)
    diag = (iota((GROUP, 16 * TILE), 0) % 16) == (iota((GROUP, 16 * TILE), 1) // TILE)

    def start_round(r, data, square):
        hi, mid, lo = split3(square)
        extra = jnp.where(lane == 0, hi, jnp.where(lane == 1, mid, jnp.where(lane == 2, lo, 0.0)))
        message = jnp.where(scalar_row, extra, data).astype(BF)
        at = pl.ds(pl.multiple_of(r * ROWS, ROWS), ROWS)
        send.reshape(ROUNDS * ROWS, TILE)[at, :] = message
        recv[r * NDEV + mine] = send[r * NDEV + mine]
        for place in others:
            pltpu.make_async_remote_copy(
                src_ref=send.at[r * NDEV + index_of(place)],
                dst_ref=recv.at[r * NDEV + mine],
                send_sem=send_sem.at[r],
                recv_sem=recv_sem.at[r],
                device_id=place,
                device_id_type=MESH,
            ).start()

    def end_round(r):
        landed = recv.at[pl.ds(r * NDEV, PEERS)]
        pltpu.make_async_copy(landed, landed, recv_sem.at[r]).wait()
        at = pl.ds(pl.multiple_of(r * ROWS, ROWS), ROWS)
        got = recv.reshape(ROUNDS * ROWS, TILE)[at, :]
        return got, total(jnp.where(scalar_mask, got.astype(F32), 0.0))

    def lhs_of(g):
        vectors = picked[pl.ds(pl.multiple_of(g * GROUP, GROUP), GROUP), :]
        return jnp.where(diag, jnp.tile(vectors, (1, 16)), zero)

    def keep(g, result):
        at = pl.multiple_of(g * GROUP, GROUP)
        split_store(parts, at, 16, result[:16, :TILE])
        split_store(parts, at + 16, 16, result[16:, TILE:])

    def adjoint_group(g):
        pair = [tiles[pl.ds(g * GROUP + 16 * h, 16)].reshape(16 * TILE, TILE) for h in range(2)]
        rhs = jnp.concatenate(pair, axis=1)
        keep(g, jnp.dot(lhs_of(g), rhs, preferred_element_type=F32))

    def forward_group(g):
        pair = []
        for h in range(2):
            block = tiles[pl.ds(g * GROUP + 16 * h, 16)]
            pair.append(jnp.concatenate([block[i] for i in range(16)], axis=1))
        rhs = jnp.concatenate(pair, axis=0)
        keep(
            g,
            lax.dot_general(
                lhs_of(g), rhs, (((1,), (1,)), ((), ())), preferred_element_type=F32
            ),
        )

    def pick_rays(uraw):
        both = jnp.concatenate([uraw, jnp.zeros_like(uraw)], axis=0).astype(BF)
        picked[...] = jnp.dot(q_row[...], both, preferred_element_type=F32).astype(BF)

    def slot_sums():
        sums = jnp.dot(s_slot[...], parts[...], preferred_element_type=F32)
        return sums[:, :TILE] + sums[:, TILE:]

    def owner_vraw(got, square, v):
        beta = jnp.sqrt(square)
        grad = jnp.dot(comb[...], got, preferred_element_type=F32)
        return beta, grad / beta - beta * v

    uraw = rays[...]
    uraw_r[...] = uraw
    v_r[...] = jnp.zeros_like(v_r)
    w_r[...] = jnp.zeros_like(w_r)
    sol[...] = jnp.zeros_like(sol)
    pick_rays(uraw)
    for g in range(NG):
        load(g).wait()
        adjoint_group(g)
    sums = slot_sums()
    pl.semaphore_wait(barrier, PEERS)
    start_round(0, sums, total(uraw * uraw))

    def iteration(k, carry):
        phibar, rhobar = carry
        got, square = end_round(2 * k)
        beta, vraw = owner_vraw(got, square, v_r[...])
        outgoing = jnp.dot(gath[...], vraw.astype(BF), preferred_element_type=F32)
        start_round(2 * k + 1, outgoing, total(vraw * vraw))
        vraw_r[...] = vraw
        u_r[...] = uraw_r[...] / beta
        got, square = end_round(2 * k + 1)
        alpha = jnp.sqrt(square)
        picked[...] = jnp.dot(p_slot[...], got, preferred_element_type=F32).astype(BF)

        def forward_step(g, c):
            forward_group(g)
            return c

        def adjoint_step(g, c):
            adjoint_group(g)
            return c

        lax.fori_loop(0, NG, forward_step, 0, unroll=4)
        both = jnp.dot(s_row[...], parts[...], preferred_element_type=F32)
        uraw = (both[:, :TILE] + both[:, TILE:]) / alpha - alpha * u_r[...]
        uraw_r[...] = uraw
        pick_rays(uraw)
        lax.fori_loop(0, NG, adjoint_step, 0, unroll=4)
        start_round(2 * k + 2, slot_sums(), total(uraw * uraw))

        first = k == 0
        v_new = vraw_r[...] / alpha
        rhobar1 = jnp.sqrt(rhobar * rhobar + DAMPING * DAMPING)
        phibar = rhobar / rhobar1 * phibar
        rho = jnp.sqrt(rhobar1 * rhobar1 + beta * beta)
        cosine = rhobar1 / rho
        sine = beta / rho
        theta = sine * alpha
        w = w_r[...]
        sol[...] += jnp.where(first, 0.0, cosine * phibar / rho) * w
        w_r[...] = v_new - jnp.where(first, 0.0, theta / rho) * w
        v_r[...] = v_new
        phibar = jnp.where(first, beta, sine * phibar)
        rhobar = jnp.where(first, alpha, -cosine * alpha)
        return phibar, rhobar

    nothing = jnp.zeros((1, 1), F32)
    phibar, rhobar = lax.fori_loop(0, ITERS, iteration, (nothing, nothing))

    got, square = end_round(2 * ITERS)
    beta, vraw = owner_vraw(got, square, v_r[...])
    start_round(2 * ITERS + 1, jnp.zeros((ROWS, TILE), F32), total(vraw * vraw))
    rhobar1 = jnp.sqrt(rhobar * rhobar + DAMPING * DAMPING)
    phibar = rhobar / rhobar1 * phibar
    rho = jnp.sqrt(rhobar1 * rhobar1 + beta * beta)
    sol[...] += rhobar1 / rho * phibar / rho * w_r[...]
    _, square = end_round(2 * ITERS + 1)
    scale = (BLK_DEV * TILE * NDEV) ** 0.5
    right[...] = vraw / jnp.sqrt(square) * scale

    def drain(r, c):
        sent = send.at[pl.ds(r * NDEV, PEERS)]
        pltpu.make_async_copy(sent, sent, send_sem.at[r]).wait()
        return c

    lax.fori_loop(0, ROUNDS, drain, 0)


def per_device(tiles, rays, tile_rows, tile_slots, tile_count, wanted):
    padded = jnp.pad(wanted[0], ((0, 0), (0, MSG - 2)), constant_values=-1).reshape(1, ROWS)
    idx = jnp.concatenate(
        [
            tile_slots.reshape(1, NT),
            tile_rows.reshape(1, NT),
            padded,
            jnp.broadcast_to(tile_count.reshape(1, 1), (5, NT)),
        ],
        axis=0,
    )
    vmem = pl.BlockSpec(memory_space=pltpu.VMEM)
    blocks = (BLK_DEV, TILE)
    return pl.pallas_call(
        kernel,
        name="lsqr",
        out_shape=(jax.ShapeDtypeStruct(blocks, F32), jax.ShapeDtypeStruct(blocks, F32)),
        in_specs=[pl.BlockSpec(memory_space=pltpu.HBM), vmem, vmem],
        out_specs=(vmem, vmem),
        scratch_shapes=[
            pltpu.VMEM((NT, TILE, TILE), BF),
            pltpu.VMEM((NT, TILE), BF),
            pltpu.VMEM((NT, 2 * TILE), BF),
            pltpu.VMEM((ROWS, NT), BF),
            pltpu.VMEM((NT, ROWS), BF),
            pltpu.VMEM((64, NT), BF),
            pltpu.VMEM((NT, TILE), BF),
            pltpu.VMEM((BLK_DEV, ROWS), BF),
            pltpu.VMEM((ROWS, BLK_DEV), BF),
            pltpu.VMEM((64, TILE), F32),
            pltpu.VMEM((64, TILE), F32),
            pltpu.VMEM(blocks, F32),
            pltpu.VMEM(blocks, F32),
            pltpu.VMEM(blocks, F32),
            pltpu.VMEM((ROUNDS * NDEV, MSG, TILE), BF),
            pltpu.VMEM((ROUNDS * NDEV, MSG, TILE), BF),
            pltpu.SemaphoreType.DMA((NG,)),
            pltpu.SemaphoreType.DMA((ROUNDS,)),
            pltpu.SemaphoreType.DMA((ROUNDS,)),
        ],
        compiler_params=pltpu.CompilerParams(
            collective_id=0, has_side_effects=True, vmem_limit_bytes=60 * 2**20
        ),
    )(tiles, rays, idx)


def solution(mesh):
    split = Mesh(mesh.devices.reshape(SIZES), AXES)
    placed = (
        P(AXES, None, None),
        P(AXES, None),
        P(AXES),
        P(AXES),
        P(AXES),
        P(AXES, None, None),
    )
    return jax.shard_map(
        per_device,
        mesh=split,
        in_specs=placed,
        out_specs=(P(AXES, None), P(AXES, None)),
        check_vma=False,
    )
```

time: 366 us -> 101 us (0.28); the launches traced: 359 us -> 100 us
  blocking collectives: 157 us -> 0 us
  Pallas kernels: 0 us -> 93.6 us
  matrix products: 68.9 us -> 0 us
  waiting for transfers between devices: 36.1 us -> 0 us
  other arithmetic: 37 us -> 1.38 us
  starting transfers between devices: 27.8 us -> 0 us
  between operations: 18.7 us -> 1.3 us
  local copies, waits for them, and re-layouts: 14.2 us -> 4.11 us
    psum x16 -> x0, blocking collectives: 129 us -> none  [over_axes(): value = lax.psum(value, axis)]
    pallas_call x0 -> x1, Pallas kernels: none -> 93.6 us  [per_device(): pl.pallas_call(kernel, name='lsqr', out_shape=(jax.ShapeDtypeStruct(block...]
    dot_general x7 -> x0, matrix products: 68.9 us -> none  [the longest x3 36.6 us: per_device(): jnp.einsum('tij,tj->ti', tiles, forward_picked, preferred_element_type=jn...]
    all_to_all x5 -> x0, waiting for transfers between devices: 36.1 us -> none  [the longest x3 18.3 us: per_device(): lax.all_to_all(outgoing, SRC_REG, split_axis=0, concat_axis=0, tiled=True)]
    all_to_all x2 -> x0, blocking collectives: 27.9 us -> none  [per_device(): lax.all_to_all(slot_sums.astype(jnp.bfloat16), SRC_REG, split_axis=0, con...]
    scatter-add x11 -> x0, other arithmetic: 27.9 us -> none  [the longest x3 12.3 us: per_device(): jax.ops.segment_sum(product, tile_rows, num_segments=row_blocks) / alpha]
    all_to_all x5 -> x0, starting transfers between devices: 27.8 us -> none  [the longest x2 16.1 us: per_device(): lax.all_to_all(slot_sums.astype(jnp.bfloat16), SRC_REG, split_axis=0, con...]
    gather x10 -> x0, local copies, waits for them, and re-layouts: 13.8 us -> none  [the longest x4 5.35 us: per_device(): picked = uraw.astype(jnp.bfloat16)[tile_rows]]
  transfers between devices with their start and end apart: 5 -> 0, of which waited for: 5 -> 0; matrix products, arithmetic and copies ran while one was open for 0% -> 0% of each run, Pallas kernels for 0% -> 0%
where the time goes in v1:
time: 101 us; the launch traced here: 100 us
  Pallas kernels  93.6 us (93%)
  local copies, waits for them, and re-layouts  4.11 us (4%)
  other arithmetic  1.38 us (1%)
  between operations  1.3 us (1%)
    pallas_call x1, Pallas kernels, per_device(): pl.pallas_call(kernel, name='lsqr', out_shape=(jax.ShapeDtypeStruct(block...  93.6 us
    unnamed x3, local copies, waits for them, and re-layouts  3.92 us

profile of v1, /device:TPU:1, one launch (start us, length us, event | category | flops | bytes accessed | tf_op | source)
XLA Modules:
  0.0 100.4 jit_solution(17952776543589011066)
XLA Ops:
  1.3 0.1 pad.8.clone
  1.4 0.8 copy.10
  2.2 0.1 reshape.17
  2.3 1.4 %add_add_fusion.idx = s32[8,512]{1,0:T(8,128)} fusion(s32[1,512]{1,0:T(1,128)S(1)} %reshape.17, s32[1,512]{1,0:T(1,128)} %bitcast.5, s32[1,512]{1,0:T(1,128)} %bitcast.6, s32[8]{0:T(128)S(1)} %pad.8.clone), kind=kLoop, calls=%fused_computation | loop fusion | flops 12288 | bytes 22560 | tf_op jit(solution)/shard_map/concatenate | solution.py:246
  3.6 93.6 %lsqr.1 = (f32[256,128]{1,0:T(8,128)}, f32[256,128]{1,0:T(8,128)}) custom-call(bf16[512,128,128]{2,1,0:T(8,128)(2,1)} %tiles_hbm.1, f32[64,128]{1,0:T(8,128)} %rays.1, s32[8,512]{1,0:T(8,128)} %add_add_fusion.idx), custom_call_target="tpu_custom_call" | custom-call | tf_op jit(solution)/shard_map/lsqr/pallas_call | solution.py:257
  97.3 1.6 %copy.14 = f32[256,128]{1,0:T(8,128)} copy(f32[256,128]{1,0:T(8,128)} %get-tuple-element.4) | data formatting | bytes 262144
  98.8 1.6 %copy.15 = f32[256,128]{1,0:T(8,128)} copy(f32[256,128]{1,0:T(8,128)} %get-tuple-element.5) | data formatting | bytes 262144
  (2 shorter events, 0.0 us)

commit v2 on v1

v2 whole, which is shorter than its diff:
```python
import jax
import jax.numpy as jnp
from jax import lax
from jax.experimental import pallas as pl
from jax.experimental.pallas import tpu as pltpu
from jax.sharding import Mesh
from jax.sharding import PartitionSpec as P

AXES = ("src_0", "src_1", "reg_0", "reg_1")
SIZES = (4, 4, 4, 2)
NDEV = 128
PEERS = NDEV - 1
BLK_DEV = 256
ITERS = 3
ROUNDS = 2 * ITERS + 2
NT = 512
TILE = 128
GROUP = 128
HALF = GROUP // 2
CHUNK = 32
FLIP = 32
MSG = 4
ROWS = NDEV * MSG
DAMPING = 0.5
BF = jnp.bfloat16
F32 = jnp.float32
MESH = pl.DeviceIdType.MESH


def peers_of(me):
    at = [
        [(me[axis] + off) % SIZES[axis] for off in range(SIZES[axis])] for axis in range(4)
    ]
    offsets = [
        (a, b, c, d) for a in range(4) for b in range(4) for c in range(4) for d in range(2)
    ]
    far = lambda o: -(min(o[0], 4 - o[0]) + min(o[1], 4 - o[1]) + min(o[2], 4 - o[2]) + o[3])
    offsets = sorted((o for o in offsets if any(o)), key=far)
    return [tuple(at[axis][o[axis]] for axis in range(4)) for o in offsets]


def index_of(place):
    return ((place[0] * 4 + place[1]) * 4 + place[2]) * 2 + place[3]


def total(x):
    return jnp.sum(jnp.sum(x, axis=0, keepdims=True), axis=1, keepdims=True)


def low_part(x):
    return x - x.astype(BF).astype(F32)


def kernel(
    tiles_hbm, rays_hbm, slots_hbm, rows_hbm, wanted_hbm, count_hbm,
    base_hbm, w_hbm, vraw_hbm, coef_hbm,
    tiles, flipped, rays, slots_r, rows_r, wanted_r, count_r,
    picked, parts, s_slot, p_slot, s_row, q_row, comb, gath, uraw_r, u_r, v_r, vraw_r, w_r, sol_r, coef_r,
    send, recv, load_sem, small_sem, out_sem, send_sem, recv_sem,
):
    me = tuple(lax.axis_index(axis) for axis in AXES)
    mine = index_of(me)
    others = peers_of(me)

    smalls = [
        pltpu.make_async_copy(src, dst, small_sem.at[i])
        for i, (src, dst) in enumerate(
            [
                (rows_hbm, rows_r),
                (rays_hbm, rays),
                (slots_hbm, slots_r),
                (count_hbm, count_r),
                (wanted_hbm, wanted_r),
            ]
        )
    ]

    def load(g):
        at = pl.ds(g * CHUNK, CHUNK)
        return pltpu.make_async_copy(tiles_hbm.at[at], tiles.at[at], load_sem.at[g])

    for copy in smalls:
        copy.start()
    for g in range(NT // CHUNK):
        load(g).start()
    barrier = pltpu.get_barrier_semaphore()
    for place in others:
        pl.semaphore_signal(barrier, inc=1, device_id=place, device_id_type=MESH)

    iota = lambda shape, dim: lax.broadcasted_iota(jnp.int32, shape, dim)
    zero = jnp.zeros((), BF)
    msg_id = iota((ROWS, TILE), 0) % MSG
    diag = (iota((GROUP, HALF * TILE), 0) % HALF) == (iota((GROUP, HALF * TILE), 1) // TILE)

    def one_hot(left, right):
        return jnp.where(left == right, 1.0, 0.0).astype(BF)

    def start_round(r, data, square):
        message = jnp.where(msg_id == 2, square, jnp.where(msg_id == 3, low_part(square), data))
        at = pl.ds(pl.multiple_of(r * ROWS, ROWS), ROWS)
        send.reshape(ROUNDS * ROWS, TILE)[at, :] = message.astype(BF)
        recv[r * NDEV + mine] = send[r * NDEV + mine]
        for place in others:
            pltpu.make_async_remote_copy(
                src_ref=send.at[r * NDEV + index_of(place)],
                dst_ref=recv.at[r * NDEV + mine],
                send_sem=send_sem.at[r],
                recv_sem=recv_sem.at[r],
                device_id=place,
                device_id_type=MESH,
            ).start()

    def end_round(r):
        landed = recv.at[pl.ds(r * NDEV, PEERS)]
        pltpu.make_async_copy(landed, landed, recv_sem.at[r]).wait()
        at = pl.ds(pl.multiple_of(r * ROWS, ROWS), ROWS)
        return recv.reshape(ROUNDS * ROWS, TILE)[at, :]

    def tile_group(source, g):
        at = g * GROUP
        lhs = jnp.where(diag, jnp.tile(picked[pl.ds(at, GROUP), :], (1, HALF)), zero)
        pair = [source[pl.ds(at + HALF * h, HALF)].reshape(HALF * TILE, TILE) for h in range(2)]
        result = jnp.dot(lhs, jnp.concatenate(pair, axis=1), preferred_element_type=F32)
        for h, part in enumerate((result[:HALF, :TILE], result[HALF:, TILE:])):
            where = pl.ds(at + HALF * h, HALF)
            parts[where, :TILE] = part.astype(BF)
            parts[where, TILE:] = low_part(part).astype(BF)

    def flip(first, count):
        def step(i, c):
            at = first + i * FLIP
            for j in range(FLIP):
                flipped[at + j] = tiles[at + j].T
            return c

        lax.fori_loop(0, count // FLIP, step, 0)

    def pick_rays(uraw):
        picked[...] = jnp.dot(q_row[...], uraw.astype(BF), preferred_element_type=F32).astype(BF)

    def both_halves(selector):
        sums = jnp.dot(selector, parts[...], preferred_element_type=F32)
        return sums[:, :TILE] + sums[:, TILE:]

    def owner_vraw(r, v):
        both = jnp.dot(comb[...], end_round(r), preferred_element_type=F32)
        beta = jnp.sqrt(both[BLK_DEV : BLK_DEV + 1, :])
        return beta, both[:BLK_DEV, :] / beta - beta * v

    smalls[0].wait()
    s_row[...] = one_hot(iota((64, NT), 0), rows_r[...])
    q_row[...] = one_hot(iota((64, NT), 0), rows_r[...]).astype(F32).T.astype(BF)
    smalls[1].wait()
    uraw = rays[...]
    uraw_r[...] = uraw
    pick_rays(uraw)
    smalls[2].wait()
    smalls[3].wait()
    target = jnp.where(msg_id < 2, (iota((ROWS, TILE), 0) // MSG) * 2 + msg_id, -1)
    live_slots = jnp.where(iota((1, NT), 1) < count_r[...], slots_r[...], -2)
    for j in range(NT // TILE):
        s_slot[:, j * TILE : (j + 1) * TILE] = one_hot(
            target, live_slots[:, j * TILE : (j + 1) * TILE]
        )
    coef_r[...] = jnp.zeros_like(coef_r)
    v_r[...] = jnp.zeros_like(v_r)
    w_r[...] = jnp.zeros_like(w_r)
    sol_r[...] = jnp.zeros_like(sol_r)
    square = total(uraw * uraw)
    per_group = GROUP // CHUNK
    for g in range(NT // GROUP):
        for c in range(per_group):
            load(g * per_group + c).wait()
        tile_group(tiles, g)
    sums = both_halves(s_slot[...])
    pl.semaphore_wait(barrier, PEERS)
    start_round(0, sums, square)

    smalls[4].wait()
    asked = jnp.concatenate([wanted_r[0:1, :], wanted_r[1:2, :]], axis=1)
    owned = one_hot(iota((BLK_DEV, 2 * NDEV), 0), asked)
    row = iota((ROWS, 2 * NDEV), 0)
    place_of = jnp.where(row % MSG < 2, (row % MSG) * NDEV + row // MSG, -1)
    spread = one_hot(place_of, iota((ROWS, 2 * NDEV), 1))
    nt = (((1,), (1,)), ((), ()))
    comb[:BLK_DEV, :] = lax.dot_general(
        owned, spread, nt, preferred_element_type=F32
    ).astype(BF)
    gath[...] = lax.dot_general(spread, owned, nt, preferred_element_type=F32).astype(BF)
    scalar_rows = jnp.logical_and(iota((16, ROWS), 0) == 0, iota((16, ROWS), 1) % MSG >= 2)
    scalar_rows = jnp.where(scalar_rows, 1.0, 0.0).astype(BF)
    comb[BLK_DEV:, :] = scalar_rows
    flip(0, NT // 2)

    def iteration(k, carry):
        phibar, rhobar = carry
        beta, vraw = owner_vraw(2 * k, v_r[...])
        outgoing = jnp.dot(gath[...], vraw.astype(BF), preferred_element_type=F32)
        start_round(2 * k + 1, outgoing, total(vraw * vraw))
        vraw_r[...] = vraw
        u_r[...] = uraw_r[...] / beta

        @pl.when(k == 0)
        def _():
            p_slot[:NT, :] = s_slot[...].T
            p_slot[NT:, :] = scalar_rows
            flip(NT // 2, NT // 2)

        both = jnp.dot(p_slot[...], end_round(2 * k + 1), preferred_element_type=F32)
        alpha = jnp.sqrt(both[NT : NT + 1, :])
        picked[...] = both[:NT, :].astype(BF)
        for g in range(NT // GROUP):
            tile_group(flipped, g)
        uraw = both_halves(s_row[...]) / alpha - alpha * u_r[...]
        uraw_r[...] = uraw
        pick_rays(uraw)
        for g in range(NT // GROUP):
            tile_group(tiles, g)
        start_round(2 * k + 2, both_halves(s_slot[...]), total(uraw * uraw))

        first = k == 0
        v_new = vraw_r[...] / alpha
        rhobar1 = jnp.sqrt(rhobar * rhobar + DAMPING * DAMPING)
        phibar = rhobar / rhobar1 * phibar
        rho = jnp.sqrt(rhobar1 * rhobar1 + beta * beta)
        cosine = rhobar1 / rho
        sine = beta / rho
        theta = sine * alpha
        w = w_r[...]
        sol_r[...] += jnp.where(first, 0.0, cosine * phibar / rho) * w
        w_r[...] = v_new - jnp.where(first, 0.0, theta / rho) * w
        v_r[...] = v_new
        phibar = jnp.where(first, beta, sine * phibar)
        rhobar = jnp.where(first, alpha, -cosine * alpha)
        return phibar, rhobar

    nothing = jnp.zeros((1, TILE), F32)
    phibar, rhobar = lax.fori_loop(0, ITERS, iteration, (nothing, nothing))

    outs = [
        pltpu.make_async_copy(src, dst, out_sem.at[i])
        for i, (src, dst) in enumerate(
            [(sol_r, base_hbm), (w_r, w_hbm), (vraw_r, vraw_hbm), (coef_r, coef_hbm)]
        )
    ]
    outs[0].start()
    outs[1].start()
    beta, vraw = owner_vraw(2 * ITERS, v_r[...])
    start_round(2 * ITERS + 1, jnp.zeros((ROWS, TILE), F32), total(vraw * vraw))
    vraw_r[...] = vraw
    outs[2].start()
    rhobar1 = jnp.sqrt(rhobar * rhobar + DAMPING * DAMPING)
    phibar = rhobar / rhobar1 * phibar
    rho = jnp.sqrt(rhobar1 * rhobar1 + beta * beta)
    coef_r[0:1, :] = rhobar1 / rho * phibar / rho

    def drain(r, c):
        sent = send.at[pl.ds(r * NDEV, PEERS)]
        pltpu.make_async_copy(sent, sent, send_sem.at[r]).wait()
        return c

    lax.fori_loop(0, ROUNDS, drain, 0)
    for copy in outs[:3]:
        copy.wait()
    both = jnp.dot(comb[BLK_DEV:, :], end_round(2 * ITERS + 1), preferred_element_type=F32)
    coef_r[1:2, :] = (BLK_DEV * TILE * NDEV) ** 0.5 / jnp.sqrt(both[0:1, :])
    outs[3].start()
    outs[3].wait()


def per_device(tiles, rays, tile_rows, tile_slots, tile_count, wanted):
    hbm = pl.BlockSpec(memory_space=pltpu.HBM)
    blocks = (BLK_DEV, TILE)
    shapes = [blocks, blocks, blocks, (8, TILE)]
    base, w, vraw, coef = pl.pallas_call(
        kernel,
        name="lsqr",
        out_shape=[jax.ShapeDtypeStruct(shape, F32) for shape in shapes],
        in_specs=[hbm] * 6,
        out_specs=[hbm] * 4,
        scratch_shapes=[
            pltpu.VMEM((NT, TILE, TILE), BF),
            pltpu.VMEM((NT, TILE, TILE), BF),
            pltpu.VMEM((64, TILE), F32),
            pltpu.VMEM((1, NT), jnp.int32),
            pltpu.VMEM((1, NT), jnp.int32),
            pltpu.VMEM((2, NDEV), jnp.int32),
            pltpu.VMEM((1, 1), jnp.int32),
            pltpu.VMEM((NT, TILE), BF),
            pltpu.VMEM((NT, 2 * TILE), BF),
            pltpu.VMEM((ROWS, NT), BF),
            pltpu.VMEM((NT + 16, ROWS), BF),
            pltpu.VMEM((64, NT), BF),
            pltpu.VMEM((NT, 64), BF),
            pltpu.VMEM((BLK_DEV + 16, ROWS), BF),
            pltpu.VMEM((ROWS, BLK_DEV), BF),
            pltpu.VMEM((64, TILE), F32),
            pltpu.VMEM((64, TILE), F32),
            pltpu.VMEM(blocks, F32),
            pltpu.VMEM(blocks, F32),
            pltpu.VMEM(blocks, F32),
            pltpu.VMEM(blocks, F32),
            pltpu.VMEM((8, TILE), F32),
            pltpu.VMEM((ROUNDS * NDEV, MSG, TILE), BF),
            pltpu.VMEM((ROUNDS * NDEV, MSG, TILE), BF),
            pltpu.SemaphoreType.DMA((NT // CHUNK,)),
            pltpu.SemaphoreType.DMA((5,)),
            pltpu.SemaphoreType.DMA((4,)),
            pltpu.SemaphoreType.DMA((ROUNDS,)),
            pltpu.SemaphoreType.DMA((ROUNDS,)),
        ],
        compiler_params=pltpu.CompilerParams(
            collective_id=0, has_side_effects=True, vmem_limit_bytes=60 * 2**20
        ),
    )(
        tiles,
        rays,
        tile_slots.reshape(1, NT),
        tile_rows.reshape(1, NT),
        wanted[0].T,
        tile_count.reshape(1, 1),
    )
    return base + coef[0:1, :] * w, vraw * coef[1:2, :]


def solution(mesh):
    split = Mesh(mesh.devices.reshape(SIZES), AXES)
    placed = (
        P(AXES, None, None),
        P(AXES, None),
        P(AXES),
        P(AXES),
        P(AXES),
        P(AXES, None, None),
    )
    return jax.shard_map(
        per_device,
        mesh=split,
        in_specs=placed,
        out_specs=(P(AXES, None), P(AXES, None)),
        check_vma=False,
    )
```

time: 101 us -> 83.8 us (0.83)
  Pallas kernels: 93.6 us -> 79.8 us
  local copies, waits for them, and re-layouts: 4.11 us -> 0.76 us
    pallas_call x1, Pallas kernels: 93.6 us -> 79.8 us  [per_device(): pl.pallas_call(kernel, name='lsqr', out_shape=[jax.ShapeDtypeStruct(shape...]
    unnamed x3 -> x0, local copies, waits for them, and re-layouts: 3.92 us -> none
    add x0 -> x1, other arithmetic: none -> 1.75 us  [per_device(): return (base + coef[0:1, :] * w, vraw * coef[1:2, :])]
    concatenate x1 -> x0, other arithmetic: 1.38 us -> none  [per_device(): jnp.concatenate([tile_slots.reshape(1, NT), tile_rows.reshape(1, NT), pad...]
where the time goes in v2:
time: 83.8 us; the launch traced here: 83.6 us
  Pallas kernels  79.8 us (95%)
  other arithmetic  1.75 us (2%)
  between operations  1.29 us (2%)
    pallas_call x1, Pallas kernels, per_device(): pl.pallas_call(kernel, name='lsqr', out_shape=[jax.ShapeDtypeStruct(shape...  79.8 us
    add x1, other arithmetic, per_device(): return (base + coef[0:1, :] * w, vraw * coef[1:2, :])  1.75 us

profile of v2, /device:TPU:1, one launch (start us, length us, event | category | flops | bytes accessed | tf_op | source)
XLA Modules:
  0.0 83.6 jit_solution(8477018111267123939)
XLA Ops:
  1.3 79.8 %lsqr.1 = (f32[256,128]{1,0:T(8,128)}, f32[256,128]{1,0:T(8,128)}, f32[256,128]{1,0:T(8,128)}, f32[8,128]{1,0:T(8,128)}) custom-call(bf16[512,128,128]{2,1,0:T(8,128)(2,1)} %tiles_hbm.1, f32[64,128]{1,0:T(8,128)} %rays_hbm.1, s32[1,512]{1,0:T(1,128)} %bitcast.11, s32[1,512]{1,0:T(1,128)} %bitcast.12, s32[2,128]{1,0:T(2,128)} %bitcast.13, ...), custom_call_target="tpu_custom_call" | custom-call | tf_op jit(solution)/shard_map/lsqr/pallas_call | solution.py:275
  81.1 0.8 slice_bitcast_fusion
  81.9 1.8 %multiply_add_fusion = (f32[256,128]{1,0:T(8,128)}, f32[256,128]{1,0:T(8,128)}) fusion(f32[256,128]{1,0:T(8,128)} %get-tuple-element.6, f32[256,128]{1,0:T(8,128)} %get-tuple-element.8, f32[128]{0:T(128)S(1)} %get-tuple-element.11, f32[256,128]{1,0:T(8,128)} %get-tuple-element.9, f32[128]{0:T(128)S(1)} %get-tuple-element.10), kind=kLoop, calls=%fused_computation | loop fusion | flops 98304 | bytes 656384 | tf_op jit(solution)/shard_map/add | solution.py:323

commit v3 on v2

--- a/solution.py
+++ b/solution.py
@@ -53,9 +53,9 @@
 
 def kernel(
     tiles_hbm, rays_hbm, slots_hbm, rows_hbm, wanted_hbm, count_hbm,
-    base_hbm, w_hbm, vraw_hbm, coef_hbm,
+    base_hbm, w_hbm, vraw_hbm, csol_hbm, cright_hbm,
     tiles, flipped, rays, slots_r, rows_r, wanted_r, count_r,
-    picked, parts, s_slot, p_slot, s_row, q_row, comb, gath, uraw_r, u_r, v_r, vraw_r, w_r, sol_r, coef_r,
+    picked, parts, s_slot, p_slot, s_row, q_row, comb, gath, uraw_r, u_r, v_r, vraw_r, w_r, sol_r, csol_r, cright_r,
     send, recv, load_sem, small_sem, out_sem, send_sem, recv_sem,
 ):
     me = tuple(lax.axis_index(axis) for axis in AXES)
@@ -162,7 +162,6 @@
         s_slot[:, j * TILE : (j + 1) * TILE] = one_hot(
             target, live_slots[:, j * TILE : (j + 1) * TILE]
         )
-    coef_r[...] = jnp.zeros_like(coef_r)
     v_r[...] = jnp.zeros_like(v_r)
     w_r[...] = jnp.zeros_like(w_r)
     sol_r[...] = jnp.zeros_like(sol_r)
@@ -240,7 +239,7 @@
     outs = [
         pltpu.make_async_copy(src, dst, out_sem.at[i])
         for i, (src, dst) in enumerate(
-            [(sol_r, base_hbm), (w_r, w_hbm), (vraw_r, vraw_hbm), (coef_r, coef_hbm)]
+            [(sol_r, base_hbm), (w_r, w_hbm), (vraw_r, vraw_hbm), (csol_r, csol_hbm), (cright_r, cright_hbm)]
         )
     ]
     outs[0].start()
@@ -252,7 +251,8 @@
     rhobar1 = jnp.sqrt(rhobar * rhobar + DAMPING * DAMPING)
     phibar = rhobar / rhobar1 * phibar
     rho = jnp.sqrt(rhobar1 * rhobar1 + beta * beta)
-    coef_r[0:1, :] = rhobar1 / rho * phibar / rho
+    csol_r[...] = rhobar1 / rho * phibar / rho
+    outs[3].start()
 
     def drain(r, c):
         sent = send.at[pl.ds(r * NDEV, PEERS)]
@@ -260,24 +260,24 @@
         return c
 
     lax.fori_loop(0, ROUNDS, drain, 0)
-    for copy in outs[:3]:
+    for copy in outs[:4]:
         copy.wait()
     both = jnp.dot(comb[BLK_DEV:, :], end_round(2 * ITERS + 1), preferred_element_type=F32)
-    coef_r[1:2, :] = (BLK_DEV * TILE * NDEV) ** 0.5 / jnp.sqrt(both[0:1, :])
-    outs[3].start()
-    outs[3].wait()
+    cright_r[...] = (BLK_DEV * TILE * NDEV) ** 0.5 / jnp.sqrt(both[0:1, :])
+    outs[4].start()
+    outs[4].wait()
 
 
 def per_device(tiles, rays, tile_rows, tile_slots, tile_count, wanted):
     hbm = pl.BlockSpec(memory_space=pltpu.HBM)
     blocks = (BLK_DEV, TILE)
-    shapes = [blocks, blocks, blocks, (8, TILE)]
-    base, w, vraw, coef = pl.pallas_call(
+    shapes = [blocks, blocks, blocks, (1, TILE), (1, TILE)]
+    base, w, vraw, coef_sol, coef_right = pl.pallas_call(
         kernel,
         name="lsqr",
         out_shape=[jax.ShapeDtypeStruct(shape, F32) for shape in shapes],
         in_specs=[hbm] * 6,
-        out_specs=[hbm] * 4,
+        out_specs=[hbm] * 5,
         scratch_shapes=[
             pltpu.VMEM((NT, TILE, TILE), BF),
             pltpu.VMEM((NT, TILE, TILE), BF),
@@ -300,12 +300,13 @@
             pltpu.VMEM(blocks, F32),
             pltpu.VMEM(blocks, F32),
             pltpu.VMEM(blocks, F32),
-            pltpu.VMEM((8, TILE), F32),
+            pltpu.VMEM((1, TILE), F32),
+            pltpu.VMEM((1, TILE), F32),
             pltpu.VMEM((ROUNDS * NDEV, MSG, TILE), BF),
             pltpu.VMEM((ROUNDS * NDEV, MSG, TILE), BF),
             pltpu.SemaphoreType.DMA((NT // CHUNK,)),
             pltpu.SemaphoreType.DMA((5,)),
-            pltpu.SemaphoreType.DMA((4,)),
+            pltpu.SemaphoreType.DMA((5,)),
             pltpu.SemaphoreType.DMA((ROUNDS,)),
             pltpu.SemaphoreType.DMA((ROUNDS,)),
         ],
@@ -320,7 +321,7 @@
         wanted[0].T,
         tile_count.reshape(1, 1),
     )
-    return base + coef[0:1, :] * w, vraw * coef[1:2, :]
+    return base + coef_sol * w, vraw * coef_right
 
 
 def solution(mesh):

time: 83.8 us -> 83 us (level)
  no operation moved by 1% of the time
where the time goes in v3:
time: 83 us; the launch traced here: 82.9 us
  Pallas kernels  79.8 us (96%)
  other arithmetic  1.76 us (2%)
  between operations  1.29 us (2%)
    pallas_call x1, Pallas kernels, per_device(): pl.pallas_call(kernel, name='lsqr', out_shape=[jax.ShapeDtypeStruct(shape...  79.8 us
    add x1, other arithmetic, per_device(): return (base + coef_sol * w, vraw * coef_right)  1.76 us

profile of v3, /device:TPU:1, one launch (start us, length us, event | category | flops | bytes accessed | tf_op | source)
XLA Modules:
  0.0 82.9 jit_solution(6566984165007168361)
XLA Ops:
  1.3 79.8 %lsqr.1 = (f32[256,128]{1,0:T(8,128)}, f32[256,128]{1,0:T(8,128)}, f32[256,128]{1,0:T(8,128)}, f32[1,128]{1,0:T(1,128)}, f32[1,128]{1,0:T(1,128)}) custom-call(bf16[512,128,128]{2,1,0:T(8,128)(2,1)} %tiles_hbm.1, f32[64,128]{1,0:T(8,128)} %rays_hbm.1, s32[1,512]{1,0:T(1,128)} %bitcast.9, s32[1,512]{1,0:T(1,128)} %bitcast.10, s32[2,128]{1,0:T(2,128)} %bitcast.11, ...), custom_call_target="tpu_custom_call" | custom-call | tf_op jit(solution)/shard_map/lsqr/pallas_call | solution.py:275
  81.1 1.8 %multiply_add_fusion = (f32[256,128]{1,0:T(8,128)}, f32[256,128]{1,0:T(8,128)}) fusion(f32[256,128]{1,0:T(8,128)} %get-tuple-element.7, f32[256,128]{1,0:T(8,128)} %get-tuple-element.9, f32[128]{0:T(128)} %bitcast.12, f32[256,128]{1,0:T(8,128)} %get-tuple-element.10, f32[128]{0:T(128)} %bitcast.13), kind=kLoop, calls=%fused_computation | loop fusion | flops 98304 | bytes 656384 | tf_op jit(solution)/shard_map/add | solution.py:324

commit v4 on v3

--- a/solution.py
+++ b/solution.py
@@ -34,7 +34,7 @@
     offsets = [
         (a, b, c, d) for a in range(4) for b in range(4) for c in range(4) for d in range(2)
     ]
-    far = lambda o: -(min(o[0], 4 - o[0]) + min(o[1], 4 - o[1]) + min(o[2], 4 - o[2]) + o[3])
+    far = lambda o: -(min(o[0], 4 - o[0]) + min(o[1], 4 - o[1]) + min(o[2], 4 - o[2]) - 0.5 * o[3])
     offsets = sorted((o for o in offsets if any(o)), key=far)
     return [tuple(at[axis][o[axis]] for axis in range(4)) for o in offsets]
 
@@ -144,8 +144,8 @@
 
     def owner_vraw(r, v):
         both = jnp.dot(comb[...], end_round(r), preferred_element_type=F32)
-        beta = jnp.sqrt(both[BLK_DEV : BLK_DEV + 1, :])
-        return beta, both[:BLK_DEV, :] / beta - beta * v
+        beta = jnp.sqrt(both[:1, :])
+        return beta, both[16:, :] / beta - beta * v
 
     smalls[0].wait()
     s_row[...] = one_hot(iota((64, NT), 0), rows_r[...])
@@ -182,13 +182,13 @@
     place_of = jnp.where(row % MSG < 2, (row % MSG) * NDEV + row // MSG, -1)
     spread = one_hot(place_of, iota((ROWS, 2 * NDEV), 1))
     nt = (((1,), (1,)), ((), ()))
-    comb[:BLK_DEV, :] = lax.dot_general(
+    comb[16:, :] = lax.dot_general(
         owned, spread, nt, preferred_element_type=F32
     ).astype(BF)
     gath[...] = lax.dot_general(spread, owned, nt, preferred_element_type=F32).astype(BF)
     scalar_rows = jnp.logical_and(iota((16, ROWS), 0) == 0, iota((16, ROWS), 1) % MSG >= 2)
     scalar_rows = jnp.where(scalar_rows, 1.0, 0.0).astype(BF)
-    comb[BLK_DEV:, :] = scalar_rows
+    comb[:16, :] = scalar_rows
     flip(0, NT // 2)
 
     def iteration(k, carry):
@@ -262,7 +262,7 @@
     lax.fori_loop(0, ROUNDS, drain, 0)
     for copy in outs[:4]:
         copy.wait()
-    both = jnp.dot(comb[BLK_DEV:, :], end_round(2 * ITERS + 1), preferred_element_type=F32)
+    both = jnp.dot(comb[:16, :], end_round(2 * ITERS + 1), preferred_element_type=F32)
     cright_r[...] = (BLK_DEV * TILE * NDEV) ** 0.5 / jnp.sqrt(both[0:1, :])
     outs[4].start()
     outs[4].wait()

time: 83 us -> 82.4 us (level)
  no operation moved by 1% of the time
where the time goes in v4:
time: 82.4 us; the launch traced here: 82.3 us
  Pallas kernels  79.2 us (96%)
  other arithmetic  1.76 us (2%)
  between operations  1.29 us (2%)
    pallas_call x1, Pallas kernels, per_device(): pl.pallas_call(kernel, name='lsqr', out_shape=[jax.ShapeDtypeStruct(shape...  79.2 us
    add x1, other arithmetic, per_device(): return (base + coef_sol * w, vraw * coef_right)  1.76 us

profile of v4, /device:TPU:1, one launch (start us, length us, event | category | flops | bytes accessed | tf_op | source)
XLA Modules:
  0.0 82.3 jit_solution(15005697175272064092)
XLA Ops:
  1.3 79.2 %lsqr.1 = (f32[256,128]{1,0:T(8,128)}, f32[256,128]{1,0:T(8,128)}, f32[256,128]{1,0:T(8,128)}, f32[1,128]{1,0:T(1,128)}, f32[1,128]{1,0:T(1,128)}) custom-call(bf16[512,128,128]{2,1,0:T(8,128)(2,1)} %tiles_hbm.1, f32[64,128]{1,0:T(8,128)} %rays_hbm.1, s32[1,512]{1,0:T(1,128)} %bitcast.9, s32[1,512]{1,0:T(1,128)} %bitcast.10, s32[2,128]{1,0:T(2,128)} %bitcast.11, ...), custom_call_target="tpu_custom_call" | custom-call | tf_op jit(solution)/shard_map/lsqr/pallas_call | solution.py:275
  80.5 1.8 %multiply_add_fusion = (f32[256,128]{1,0:T(8,128)}, f32[256,128]{1,0:T(8,128)}) fusion(f32[256,128]{1,0:T(8,128)} %get-tuple-element.7, f32[256,128]{1,0:T(8,128)} %get-tuple-element.9, f32[128]{0:T(128)} %bitcast.12, f32[256,128]{1,0:T(8,128)} %get-tuple-element.10, f32[128]{0:T(128)} %bitcast.13), kind=kLoop, calls=%fused_computation | loop fusion | flops 98304 | bytes 656384 | tf_op jit(solution)/shard_map/add | solution.py:324
